TPU v7x, 256 devices: a 2x2x32 block of a 4x8x32 slice. The times are simulated.
256 devices in a mesh: groups: 4 (over y, x), expert: 32 (over z), seq: 2 (over core).
Axes of the slice: x: 2, y: 2, z: 32, core: 2. Of those that a mesh axis runs over, the one named last changes fastest.
The devices are a block of a 4x8x32 slice.
Arguments:
- query: bfloat16 [128, 128, 1024], P(('groups', 'expert')), parts along dimension 0, may hold values from -160 to 160
- key_cache: bfloat16 [128, 768, 1024], P(('groups', 'expert'), 'seq'), parts along dimension 0, may hold values from -4 to 4
- value_cache: bfloat16 [128, 768, 1024], P(('groups', 'expert'), 'seq'), parts along dimension 0, may hold values from -6 to 6
- key_new: bfloat16 [128, 128, 1024], P(('groups', 'expert')), parts along dimension 0, may hold values from -6 to 6
- value_new: bfloat16 [128, 128, 1024], P(('groups', 'expert')), parts along dimension 0, may hold values from -6 to 6
- resid: bfloat16 [128, 128, 1024], P(('groups', 'expert')), parts along dimension 0, may hold values from -6 to 6
- routing: int32 [128, 128, 1], P(('groups', 'expert')), parts along dimension 0, may hold values from 0 to 31; in each aligned block of 128 rows (0 to 127, 128 to 255, ..., all dimensions but the last counted through in order) at most 12 rows name the same one
- router_prob: float32 [128, 128], P(('groups', 'expert')), parts along dimension 0, may hold values from 0.2 to 1
- out_weight: bfloat16 [1024, 1024], replicated, may hold values from -0.1875 to 0.1875
- ffn_gain: float32 [1024], replicated, may hold values from 0.5 to 2
- w_gate: bfloat16 [32, 1024, 2560], P('expert', None, 'seq'), may hold values from -0.1875 to 0.1875
- w_up: bfloat16 [32, 1024, 2560], P('expert', None, 'seq'), may hold values from -0.1875 to 0.1875
- w_down: bfloat16 [32, 2560, 1024], P('expert', 'seq'), may hold values from -0.125 to 0.125
Outputs:
- layer_out: bfloat16 [128, 128, 1024], P(('groups', 'expert')), parts along dimension 0
There are 4 independent parts, one for each index of `groups`. A program takes and returns all parts, laid end to end along the dimension named above; an argument that names none is the same for every part. Nothing has to cross between parts.
Inputs may be any that keep to these rules, and one draw needn't show every extreme that they name: `routing`: among the 128 tokens of one sequence no expert is named more than 12 times, a bound that some block reaches.
All inputs are finite; a program needn't handle non-finite values.
Results may differ from a plain program's by a relative error of at most 0.014.
Values may be sent and summed in bfloat16 or wider, within the bound.
A program may use at most 64 MiB of HBM per device.

v0:
```python
import math

import jax
import jax.numpy as jnp
from jax import lax
from jax.sharding import PartitionSpec as P

HEADS = 16
HEAD_DIM = 64


def copy_for_each(array, axis):
    copies = jnp.broadcast_to(array, (lax.axis_size(axis), *array.shape))
    return lax.all_to_all(copies, axis, split_axis=0, concat_axis=0, tiled=True)


def folded_in_pairs(pieces, combine):
    while len(jax.tree.leaves(pieces)[0]) > 1:
        pieces = jax.vmap(combine)(
            *(jax.tree.map(lambda part: part[side::2], pieces) for side in (0, 1))
        )
    return jax.tree.map(lambda part: part[0], pieces)


def combined_all(array, axis, combine):
    pieces = jax.tree.map(lambda part: copy_for_each(part, axis), array)
    return folded_in_pairs(pieces, combine)


def split_up(array, dim, peers):
    before, after = (array.shape[:dim], array.shape[dim + 1 :])
    return jnp.moveaxis(array.reshape(*before, peers, -1, *after), dim, 0)


def sum_at_owner(array, axis, dim):
    blocks = split_up(array, dim, lax.axis_size(axis))
    arrived = lax.all_to_all(blocks, axis, split_axis=0, concat_axis=0, tiled=True)
    return arrived.astype(jnp.float32).sum(axis=0)


def laid_out(blocks, dim):
    lengths = list(blocks.shape[1:])
    lengths[dim] *= blocks.shape[0]
    return jnp.moveaxis(blocks, 0, dim).reshape(lengths)


def gather_directly(array, axis, dim):
    return laid_out(copy_for_each(array, axis), dim)


def rescale(weighted, factor):
    token_rows = weighted.shape[0]
    shaped = weighted.reshape(token_rows, HEADS, HEAD_DIM) * jnp.transpose(factor)[:, :, None]
    return shaped.reshape(token_rows, HEADS * HEAD_DIM)


def join(first, runner_expert):
    peak = jnp.maximum(first[0], runner_expert[0])
    left = jnp.exp(first[0] - peak)
    right = jnp.exp(runner_expert[0] - peak)
    denom = first[1] * left + runner_expert[1] * right
    weighted = rescale(first[2], left) + rescale(runner_expert[2], right)
    return (peak, denom, weighted)


def partial_attend(heads_q, keys, values, allowed):
    scale = 1.0 / math.sqrt(HEAD_DIM)
    keys_h = keys.reshape(-1, HEADS, HEAD_DIM)
    values_h = values.reshape(-1, HEADS, HEAD_DIM)
    scores = jnp.einsum("qhd,khd->hqk", heads_q, keys_h, preferred_element_type=jnp.float32) * scale
    if allowed is not None:
        scores = jnp.where(allowed[None], scores, -jnp.inf)
    peak = jnp.max(scores, axis=2)
    expw = jnp.exp(scores - peak[:, :, None])
    denom = jnp.sum(expw, axis=2)
    weights = expw.astype(jnp.bfloat16)
    weighted = jnp.einsum("hqk,khd->qhd", weights, values_h, preferred_element_type=jnp.float32)
    return (peak, denom, weighted.reshape(heads_q.shape[0], HEADS * HEAD_DIM))


def on_device(
    query,
    key_cache,
    value_cache,
    key_new,
    value_new,
    resid,
    routing,
    router_prob,
    out_weight,
    ffn_gain,
    w_gate,
    w_up,
    w_down,
):
    tokens = query.shape[1]
    width = query.shape[2]
    heads_q = query[0].reshape(tokens, HEADS, HEAD_DIM)
    cached = partial_attend(heads_q, key_cache[0], value_cache[0], None)
    merged = combined_all(cached, "seq", join)
    causal = jnp.arange(tokens)[None, :] <= jnp.arange(tokens)[:, None]
    fresh = partial_attend(heads_q, key_new[0], value_new[0], causal)
    final = join(merged, fresh)
    attn = rescale(final[2], 1.0 / final[1]).astype(jnp.bfloat16)
    projected = jnp.dot(attn, out_weight, preferred_element_type=jnp.float32)
    hidden = (resid[0].astype(jnp.float32) + projected).astype(jnp.bfloat16)
    hidden_f = hidden.astype(jnp.float32)
    meansq = jnp.mean(hidden_f * hidden_f, axis=-1, keepdims=True)
    normed = (hidden_f * lax.rsqrt(meansq + 1e-06) * ffn_gain).astype(jnp.bfloat16)
    experts = lax.axis_size("expert")
    capacity = max(2, 3 * tokens // experts)
    route = routing[0, :, 0]
    onehot = (route[:, None] == jnp.arange(experts, dtype=jnp.int32)[None, :]).astype(jnp.float32)
    lower = (jnp.arange(tokens)[None, :] <= jnp.arange(tokens)[:, None]).astype(jnp.float32)
    running = jnp.dot(lower, onehot, preferred_element_type=jnp.float32)
    rank = (jnp.sum(running * onehot, axis=1) - 1.0).astype(jnp.int32)
    target = route * capacity + rank
    placer = (jnp.arange(experts * capacity, dtype=jnp.int32)[:, None] == target[None, :]).astype(
        jnp.bfloat16
    )
    outgoing = jnp.dot(placer, normed, preferred_element_type=jnp.float32).astype(jnp.bfloat16)
    outgoing = outgoing.reshape(experts, capacity, width)
    arrived = lax.all_to_all(outgoing, "expert", split_axis=0, concat_axis=0, tiled=True)
    sources, count, features = arrived.shape
    token_rows = arrived.reshape(sources * count, features)
    gate = jnp.dot(token_rows, w_gate[0], preferred_element_type=jnp.float32)
    upper = jnp.dot(token_rows, w_up[0], preferred_element_type=jnp.float32)
    act = (jax.nn.gelu(gate, approximate=True) * upper).astype(jnp.bfloat16)
    expert_result = jnp.dot(act, w_down[0], preferred_element_type=jnp.float32).reshape(
        sources, count, features
    )
    finished = sum_at_owner(expert_result.astype(jnp.bfloat16), "seq", 2).astype(jnp.bfloat16)
    share = lax.all_to_all(finished, "expert", split_axis=0, concat_axis=0, tiled=True)
    returned = gather_directly(share, "seq", 2)
    returned = returned.reshape(experts * capacity, width)
    expert_out = jnp.einsum("sq,sd->qd", placer, returned, preferred_element_type=jnp.float32)
    result = hidden_f + router_prob[0][:, None] * expert_out
    return result.astype(jnp.bfloat16)[None]


def solution(mesh):
    in_specs = (
        P(("groups", "expert"), None, None),
        P(("groups", "expert"), "seq", None),
        P(("groups", "expert"), "seq", None),
        P(("groups", "expert"), None, None),
        P(("groups", "expert"), None, None),
        P(("groups", "expert"), None, None),
        P(("groups", "expert"), None, None),
        P(("groups", "expert"), None),
        P(),
        P(),
        P("expert", None, "seq"),
        P("expert", None, "seq"),
        P("expert", "seq", None),
    )
    out_specs = P(("groups", "expert"), None, None)
    return jax.shard_map(
        on_device, mesh=mesh, in_specs=in_specs, out_specs=out_specs, check_vma=False
    )
```

profile of v0, /device:TPU:37, one launch (start us, length us, event | category | flops | bytes accessed | tf_op | source)
XLA Modules:
  0.0 280.0 jit_solution(16837225857219137180)
XLA Ops:
  0.0 1.9 copy.40
  1.9 1.5 copy.41
  3.5 3.2 %multiply_reduce_fusion = (f32[16,128]{1,0:T(8,128)S(1)}, f32[16,128,384]{2,1,0:T(8,128)}) fusion(bf16[128,16,64]{0,2,1:T(8,128)(2,1)} %bitcast.109, bf16[384,16,64]{0,2,1:T(8,128)(2,1)S(1)} %bitcast.103), kind=kOutput, calls=%fused_computation.2 | convolution fusion | flops 102234112 | bytes 4202496 | tf_op jit(solution)/shard_map/qhd,khd->hqk/dot_general | solution.py:70
  7.3 23.7 %all-to-all-start.1 = ((f32[2,16,128]{2,1,0:T(8,128)}), f32[2,16,128]{2,1,0:T(8,128)S(1)}, u32[]{:S(2)}, u32[]{:S(2)}) async-start(f32[2,16,128]{2,1,0:T(8,128)} %broadcast_in_dim.23), calls=%async_computation.1 | async-start | bytes 32768 | tf_op jit(solution)/shard_map/all_to_all | solution.py:14
  31.1 1.8 copy.43
  32.9 1.8 copy.44
  34.7 1.5 copy.42
  36.2 2.9 %fusion.6 = f32[16,128]{1,0:T(8,128)S(1)} fusion(f32[16,128,384]{2,1,0:T(8,128)} %get-tuple-element.14, f32[16,128]{1,0:T(8,128)S(1)} %get-tuple-element.13), kind=kLoop, calls=%fused_computation.10 | loop fusion | flops 2357248 | bytes 3162112 | tf_op jit(solution)/shard_map/reduce_sum | solution.py:75
  39.1 1.7 fusion.17
  42.9 3.3 %all-to-all-start.2 = ((f32[2,16,128]{2,1,0:T(8,128)}), f32[2,16,128]{2,1,0:T(8,128)S(1)}, u32[]{:S(2)}, u32[]{:S(2)}) async-start(f32[2,16,128]{2,1,0:T(8,128)} %broadcast_in_dim.26), calls=%async_computation.2 | async-start | bytes 32768 | tf_op jit(solution)/shard_map/all_to_all | solution.py:14
  48.3 4.8 %all-to-all-start = ((f32[2,128,1024]{1,2,0:T(8,128)}), f32[2,128,1024]{1,2,0:T(8,128)}, u32[]{:S(2)}, u32[]{:S(2)}) async-start(f32[2,128,1024]{1,2,0:T(8,128)} %broadcast_in_dim.22), calls=%async_computation | async-start | bytes 2097152 | tf_op jit(solution)/shard_map/all_to_all | solution.py:14
  53.1 1.9 all-to-all-done
  56.4 1.5 fusion.30
  57.9 1.5 multiply_reduce_fusion.1
  60.8 2.1 reshape.88
  62.9 118.1 %all_to_all.35 = bf16[32,12,1024]{2,1,0:T(8,128)(2,1)} all-to-all(bf16[32,12,1024]{2,1,0:T(8,128)(2,1)} %reshape.88), channel_id=1, replica_groups=mesh['groups'=4,'expert'=32,'seq'=2] {'expert'}, dimensions={0} | all-to-all | bytes 1572864 | tf_op jit(solution)/shard_map/all_to_all | solution.py:123
  181.1 2.1 reshape.89
  183.2 2.7 fusion.14
  185.8 2.2 fusion
  188.0 2.2 dot_general.44
  190.2 3.3 %fusion.21 = bf16[32,12,1024]{2,0,1:T(8,128)(2,1)S(1)} fusion(bf16[1,1280,1024]{2,1,0:T(8,128)(2,1)} %param.25, bf16[32,12,1280]{2,1,0:T(8,128)(2,1)} %dot_general.44), kind=kOutput, calls=%fused_computation.22 | convolution fusion | flops 1007026176 | bytes 4390912 | tf_op jit(solution)/shard_map/dot_general | solution.py:129
  193.6 5.5 %all_to_all.36 = bf16[2,32,12,512]{3,1,2,0:T(8,128)(2,1)} all-to-all(bf16[2,32,12,512]{3,1,2,0:T(8,128)(2,1)S(1)} %bitcast.104), channel_id=1, replica_groups=mesh['groups'=4,'expert'=32,'seq'=2] {'seq'}, dimensions={0} | all-to-all | bytes 1572864 | tf_op jit(solution)/shard_map/all_to_all | solution.py:37
  200.7 71.5 %all_to_all.37 = bf16[32,12,512]{2,1,0:T(8,128)(2,1)S(1)} all-to-all(bf16[32,12,512]{2,1,0:T(8,128)(2,1)S(1)} %copy.49), channel_id=1, replica_groups=mesh['groups'=4,'expert'=32,'seq'=2] {'expert'}, dimensions={0} | all-to-all | bytes 786432 | tf_op jit(solution)/shard_map/all_to_all | solution.py:133
  272.5 5.4 %all_to_all.38 = bf16[2,32,12,512]{3,1,2,0:T(8,128)(2,1)S(1)} all-to-all(bf16[2,32,12,512]{3,1,2,0:T(8,128)(2,1)S(1)} %broadcast_in_dim.27), channel_id=1, replica_groups=mesh['groups'=4,'expert'=32,'seq'=2] {'seq'}, dimensions={0} | all-to-all | bytes 1572864 | tf_op jit(solution)/shard_map/all_to_all | solution.py:14
  (50 shorter events, 11.7 us)
Async XLA Ops:
  0.0 183.2 %copy-start = (bf16[1,1024,1280]{2,1,0:T(8,128)(2,1)S(1)}, bf16[1,1024,1280]{2,1,0:T(8,128)(2,1)}, u32[]{:S(2)}) copy-start(bf16[1,1024,1280]{2,1,0:T(8,128)(2,1)} %param.23) | copy-start | bytes 7864324
  1.9 29.0 %copy-start.12 = (s32[1,128,1]{1,2,0:T(1,128)S(1)}, s32[1,128,1]{1,2,0:T(1,128)}, u32[]{:S(2)}) copy-start(s32[1,128,1]{1,2,0:T(1,128)} %param.19) | copy-start | bytes 1540
  7.3 35.0 %all-to-all-start.1 = ((f32[2,16,128]{2,1,0:T(8,128)}), f32[2,16,128]{2,1,0:T(8,128)S(1)}, u32[]{:S(2)}, u32[]{:S(2)}) async-start(f32[2,16,128]{2,1,0:T(8,128)} %broadcast_in_dim.23), calls=%async_computation.1 | async-start | bytes 32768 | tf_op jit(solution)/shard_map/all_to_all | solution.py:14
  36.2 2.9 %copy-start.1 = (f32[16,128,384]{2,1,0:T(8,128)S(1)}, f32[16,128,384]{2,1,0:T(8,128)}, u32[]{:S(2)}) copy-start(f32[16,128,384]{2,1,0:T(8,128)} %get-tuple-element.14) | copy-start | bytes 9437188
  39.1 1.8 copy-start.3
  39.1 1.8 copy-start.6
  40.8 6.4 %copy-start.4 = (f32[16,128,64]{1,2,0:T(8,128)S(1)}, f32[16,128,64]{1,2,0:T(8,128)}, u32[]{:S(2)}) copy-start(f32[16,128,64]{1,2,0:T(8,128)} %fusion.17) | copy-start | bytes 1572868
  41.2 1.0 copy-start.2
  42.9 4.3 %all-to-all-start.2 = ((f32[2,16,128]{2,1,0:T(8,128)}), f32[2,16,128]{2,1,0:T(8,128)S(1)}, u32[]{:S(2)}, u32[]{:S(2)}) async-start(f32[2,16,128]{2,1,0:T(8,128)} %broadcast_in_dim.26), calls=%async_computation.2 | async-start | bytes 32768 | tf_op jit(solution)/shard_map/all_to_all | solution.py:14
  47.2 9.1 %copy-start.7 = (bf16[1,128,1024]{1,2,0:T(8,128)(2,1)S(1)}, bf16[1,128,1024]{1,2,0:T(8,128)(2,1)}, u32[]{:S(2)}) copy-start(bf16[1,128,1024]{1,2,0:T(8,128)(2,1)} %copy.44) | copy-start | bytes 786436
  48.3 6.6 %all-to-all-start = ((f32[2,128,1024]{1,2,0:T(8,128)}), f32[2,128,1024]{1,2,0:T(8,128)}, u32[]{:S(2)}, u32[]{:S(2)}) async-start(f32[2,128,1024]{1,2,0:T(8,128)} %broadcast_in_dim.22), calls=%async_computation | async-start | bytes 2097152 | tf_op jit(solution)/shard_map/all_to_all | solution.py:14
  54.9 3.0 %copy-start.5 = (bf16[1024,1024]{1,0:T(8,128)(2,1)S(1)}, bf16[1024,1024]{1,0:T(8,128)(2,1)}, u32[]{:S(2)}) copy-start(bf16[1024,1024]{1,0:T(8,128)(2,1)} %param.21) | copy-start | bytes 6291460
  56.4 3.1 %copy-start.9 = (f32[1024]{0:T(1024)S(1)}, f32[1024]{0:T(1024)}, u32[]{:S(2)}) copy-start(f32[1024]{0:T(1024)} %param.22) | copy-start | bytes 12292
  183.2 2.7 copy-start.8
  183.2 2.7 copy-start.11
  272.5 6.4 %copy-start.10 = (f32[1,128]{1,0:T(1,128)S(1)}, f32[1,128]{1,0:T(1,128)}, u32[]{:S(2)}) copy-start(f32[1,128]{1,0:T(1,128)} %param.20) | copy-start | bytes 1540
where the time goes:
time: 281 us; the launch traced here: 280 us
  blocking collectives  201 us (72%)
  starting transfers between devices  31.7 us (11%)
  local copies, waits for them, and re-layouts  19.7 us (7%)
  matrix products  19 us (7%)
  other arithmetic  5.8 us (2%)
  waiting for transfers between devices  2.87 us (1%)
    all_to_all x1, blocking collectives, on_device(): lax.all_to_all(outgoing, 'expert', split_axis=0, concat_axis=0, tiled=True)  118 us
    all_to_all x1, blocking collectives, on_device(): lax.all_to_all(finished, 'expert', split_axis=0, concat_axis=0, tiled=True)  71.5 us
    all_to_all x3, starting transfers between devices, copy_for_each(): return lax.all_to_all(copies, axis, split_axis=0, concat_axis=0, tiled=True)  31.7 us
    unnamed x32, local copies, waits for them, and re-layouts  9.64 us
  transfers between devices with their start and end apart: 3, of which 2 were waited for; matrix products, arithmetic and copies ran while one was open for 4% of the time, Pallas kernels for 0%

commit v1 on v0

v1 whole, which is shorter than its diff:
```python
import functools
import math

import jax
import jax.numpy as jnp
from jax import lax
from jax.experimental import pallas as pl
from jax.experimental.pallas import tpu as pltpu
from jax.sharding import PartitionSpec as P

HEAD_DIM = 64
LANES = 128
GROUP = 8
MESH = pl.DeviceIdType.MESH
NEG = -1e30


def iota(shape, dim):
    return lax.broadcasted_iota(jnp.int32, shape, dim)


def dot(a, b):
    return jnp.dot(a, b, preferred_element_type=jnp.float32)


def dot_t(a, b):
    return lax.dot_general(a, b, (((1,), (1,)), ((), ())), preferred_element_type=jnp.float32)


def attention_kernel(
    query, key_cache, value_cache, key_new, value_new, resid, out_weight, gain,
    hidden_ref, normed_ref,
    q_v, k_v, v_v, r_v, w_v, sums, stats, sums_in, stats_in, attn,
    copy_sem, send_sem, recv_sem,
):
    core = lax.axis_index("seq")
    other = {"seq": 1 - core}
    tokens, width = q_v.shape
    cached = key_cache.shape[0]
    keys = k_v.shape[0]
    pairs = width // LANES
    fresh_half = tokens // 2

    barrier = pltpu.get_barrier_semaphore()
    pl.semaphore_signal(barrier, inc=1, device_id=other, device_id_type=MESH)
    loads = [
        pltpu.make_async_copy(src, dst, copy_sem.at[i])
        for i, (src, dst) in enumerate([
            (query, q_v),
            (key_cache, k_v.at[pl.ds(0, cached)]),
            (key_new, k_v.at[pl.ds(cached, tokens)]),
            (value_cache, v_v.at[pl.ds(0, cached)]),
            (value_new, v_v.at[pl.ds(cached, tokens)]),
            (out_weight, w_v),
            (resid, r_v),
        ])
    ]
    for load in loads:
        load.start()
    stats[...] = jnp.zeros_like(stats)
    pl.semaphore_wait(barrier, 1)
    for load in loads[:5]:
        load.wait()

    def to_other(pair):
        return pltpu.make_async_remote_copy(
            src_ref=sums.at[pair], dst_ref=sums_in.at[pair],
            send_sem=send_sem.at[pair], recv_sem=recv_sem.at[pair],
            device_id=other, device_id_type=MESH,
        )

    low = iota((tokens, LANES), 1) < HEAD_DIM
    lane = iota((tokens, LANES), 1)
    col = iota((2 * tokens, keys), 1) - cached
    row = lax.rem(iota((2 * tokens, keys), 0), tokens)
    mine = lax.div(jnp.maximum(col, 0), fresh_half) == core
    allowed = (col < 0) | ((col <= row) & mine)

    def one_pair(pair, carry):
        lanes = pl.ds(pl.multiple_of(pair * LANES, LANES), LANES)
        q = q_v[:, lanes] * jnp.bfloat16(1.0 / math.sqrt(HEAD_DIM))
        zero = jnp.zeros_like(q)
        both = jnp.concatenate([jnp.where(low, q, zero), jnp.where(low, zero, q)], axis=0)
        scores = jnp.where(allowed, dot_t(both, k_v[:, lanes]), NEG)
        peak = jnp.max(scores, axis=1, keepdims=True)
        expw = jnp.exp(scores - peak)
        denom = jnp.sum(expw, axis=1, keepdims=True)
        weighted = dot(expw.astype(jnp.bfloat16), v_v[:, lanes])
        sums[pair] = jnp.where(low, weighted[:tokens], weighted[tokens:])
        kept = stats[...]
        for side in range(2):
            rows = slice(side * tokens, (side + 1) * tokens)
            head = 2 * pair + side
            kept = jnp.where(lane == head, peak[rows], kept)
            kept = jnp.where(lane == head + 2 * pairs, denom[rows], kept)
        stats[...] = kept
        to_other(pair).start()
        return carry

    lax.fori_loop(0, pairs, one_pair, 0)
    stat_copy = pltpu.make_async_remote_copy(
        src_ref=stats, dst_ref=stats_in, send_sem=send_sem.at[pairs], recv_sem=recv_sem.at[pairs],
        device_id=other, device_id_type=MESH,
    )
    stat_copy.start()
    stat_copy.wait()

    for pair in range(pairs):
        to_other(pair).wait()
        own, their = stats[...], stats_in[...]
        spread = []
        for kind in (own, their):
            for offset in (0, 2 * pairs):
                spots = [kind[:, offset + 2 * pair + side : offset + 2 * pair + side + 1] for side in range(2)]
                spread.append(jnp.where(low, spots[0], spots[1]))
        peak = jnp.maximum(spread[0], spread[2])
        left, right = jnp.exp(spread[0] - peak), jnp.exp(spread[2] - peak)
        denom = spread[1] * left + spread[3] * right
        total = sums[pair] * left + sums_in[pair] * right
        attn[:, pair * LANES : (pair + 1) * LANES] = (total / denom).astype(jnp.bfloat16)

    loads[5].wait()
    loads[6].wait()
    hidden = (r_v[...].astype(jnp.float32) + dot(attn[...], w_v[...])).astype(jnp.bfloat16)
    hidden_ref[...] = hidden
    hidden_f = hidden.astype(jnp.float32)
    meansq = jnp.mean(hidden_f * hidden_f, axis=1, keepdims=True)
    normed_ref[...] = (hidden_f * lax.rsqrt(meansq + 1e-06) * gain[...]).astype(jnp.bfloat16)


def expert_kernel(
    peers, cap,
    normed, hidden, route_col, route_row, prob, w_gate, w_up, w_down,
    out,
    wg, wu, wd, outgoing, arrived, results, returned, total, part, part_in, shuffle, shuffle_t,
    copy_sem, wsend_sem, wrecv_sem, send_sem, recv_sem, back_send, back_recv, last_sem,
):
    me = lax.axis_index("expert")
    core = lax.axis_index("seq")
    other = {"seq": 1 - core}
    tokens, width = normed.shape
    blocks = width // LANES
    slots = cap // 2
    rows = slots * blocks
    group_tokens = GROUP * slots
    group_rows = GROUP * rows
    groups = peers // GROUP
    half = peers // 2
    rels = [half + ((n + 1) // 2) * (1 - 2 * (n % 2)) for n in range(peers)]

    barrier = pltpu.get_barrier_semaphore()
    for rel in rels[:-1]:
        pl.semaphore_signal(barrier, inc=1, device_id={"expert": lax.rem(me + rel, peers)}, device_id_type=MESH)
    pl.semaphore_signal(barrier, inc=1, device_id=other, device_id_type=MESH)
    loads = [
        pltpu.make_async_copy(src, dst.at[0], copy_sem.at[i])
        for i, (src, dst) in enumerate([(w_gate, wg), (w_up, wu), (w_down, wd)])
    ]
    for load in loads:
        load.start()

    same = route_col[...] == route_row[...]
    first, second = iota((tokens, tokens), 0), iota((tokens, tokens), 1)

    def place(route, rank):
        delta = lax.rem(route - me + peers, peers) - half
        order = jnp.where(delta > 0, 2 * delta, jnp.maximum(-2 * delta - 1, 0))
        slot = rank - core * slots
        return jnp.where((slot >= 0) & (slot < slots), order * slots + slot, -1)

    place_col = place(route_col[...], jnp.sum(jnp.where(same & (second < first), 1, 0), axis=1, keepdims=True))
    place_row = place(route_row[...], jnp.sum(jnp.where(same & (first < second), 1, 0), axis=0, keepdims=True))

    def moves(packed, plain):
        peer, block, slot = packed // rows, lax.rem(packed, rows) // slots, lax.rem(packed, slots)
        return jnp.where(plain == block * group_tokens + peer * slots + slot, 1.0, 0.0).astype(jnp.bfloat16)

    square = (group_rows, group_rows)
    shuffle[...] = moves(iota(square, 1), iota(square, 0))
    shuffle_t[...] = moves(iota(square, 0), iota(square, 1))

    def pack(values):
        stacked = jnp.concatenate([values[:, j * LANES : (j + 1) * LANES] for j in range(blocks)], axis=0)
        return dot(shuffle_t[...], stacked).astype(jnp.bfloat16)

    def unpack(packed):
        plain = dot(shuffle[...], packed).astype(jnp.bfloat16)
        return jnp.concatenate(
            [plain[j * group_tokens : (j + 1) * group_tokens] for j in range(blocks)], axis=1
        )

    for g in range(groups):
        picked = jnp.where(
            place_row == g * group_tokens + iota((group_tokens, tokens), 0), 1.0, 0.0
        ).astype(jnp.bfloat16)
        chosen = dot(picked, normed[...]).astype(jnp.bfloat16)
        outgoing[pl.ds(g * group_rows, group_rows)] = pack(chosen)
    own = pl.ds((peers - 1) * rows, rows)
    arrived[own] = outgoing[own]

    pl.semaphore_wait(barrier, peers)
    sends = []
    for n in range(peers - 1):
        spot = pl.ds(n * rows, rows)
        sends.append(pltpu.make_async_remote_copy(
            src_ref=outgoing.at[spot], dst_ref=arrived.at[spot], send_sem=send_sem.at[n], recv_sem=recv_sem.at[n],
            device_id={"expert": lax.rem(me + rels[n], peers)}, device_id_type=MESH,
        ))
        sends[-1].start()
    halves = [
        pltpu.make_async_remote_copy(
            src_ref=src, dst_ref=dst.at[1], send_sem=wsend_sem.at[i], recv_sem=wrecv_sem.at[i],
            device_id=other, device_id_type=MESH,
        )
        for i, (src, dst) in enumerate([(w_gate, wg), (w_up, wu), (w_down, wd)])
    ]
    for copy in halves:
        copy.start()
    for load in loads:
        load.wait()
    for copy in halves:
        copy.wait_recv()

    chunk = 2 * LANES
    chunks = wg.shape[2] // chunk
    backs = []
    for g in range(groups):
        for n in range(g * GROUP, min((g + 1) * GROUP, peers - 1)):
            sends[n].wait_recv()
        rows_in = unpack(arrived[pl.ds(g * group_rows, group_rows)])
        total[...] = jnp.zeros_like(total)

        def step(k, carry, rows_in=rows_in):
            side, at = k // chunks, pl.multiple_of(lax.rem(k, chunks) * chunk, chunk)
            gate = dot(rows_in, wg[side, :, pl.ds(at, chunk)])
            upper = dot(rows_in, wu[side, :, pl.ds(at, chunk)])
            act = (jax.nn.gelu(gate, approximate=True) * upper).astype(jnp.bfloat16)
            total[...] += dot(act, wd[side, pl.ds(at, chunk), :])
            return carry

        lax.fori_loop(0, 2 * chunks, step, 0)
        results[pl.ds(g * group_rows, group_rows)] = pack(total[...].astype(jnp.bfloat16))
        for n in range(g * GROUP, min((g + 1) * GROUP, peers - 1)):
            spot = pl.ds(n * rows, rows)
            backs.append(pltpu.make_async_remote_copy(
                src_ref=results.at[spot], dst_ref=returned.at[spot], send_sem=back_send.at[n], recv_sem=back_recv.at[n],
                device_id={"expert": lax.rem(me + peers - rels[n], peers)}, device_id_type=MESH,
            ))
            backs[-1].start()
    returned[own] = results[own]

    summed = jnp.zeros((tokens, width), jnp.float32)
    for g in range(groups):
        for n in range(g * GROUP, min((g + 1) * GROUP, peers - 1)):
            backs[n].wait_recv()
        rows_back = unpack(returned[pl.ds(g * group_rows, group_rows)])
        picked = jnp.where(
            place_col == g * group_tokens + iota((tokens, group_tokens), 1), 1.0, 0.0
        ).astype(jnp.bfloat16)
        summed += dot(picked, rows_back)
    part[...] = summed.astype(jnp.bfloat16)
    last = pltpu.make_async_remote_copy(
        src_ref=part, dst_ref=part_in, send_sem=last_sem.at[0], recv_sem=last_sem.at[1],
        device_id=other, device_id_type=MESH,
    )
    last.start()
    last.wait_recv()
    expert_out = summed + part_in[...].astype(jnp.float32)
    out[...] = (hidden[...].astype(jnp.float32) + prob[...] * expert_out).astype(jnp.bfloat16)
    for copy in sends + halves + backs + [last]:
        copy.wait_send()


ANY = pl.BlockSpec(memory_space=pl.ANY)
VMEM = pl.BlockSpec(memory_space=pltpu.VMEM)


def on_device(
    peers, query, key_cache, value_cache, key_new, value_new, resid, routing, router_prob,
    out_weight, ffn_gain, w_gate, w_up, w_down,
):
    tokens, width = query.shape[1:]
    cached = key_cache.shape[1]
    keys = cached + tokens
    pairs = width // LANES
    bf16, f32 = jnp.bfloat16, jnp.float32
    hidden, normed = pl.pallas_call(
        attention_kernel,
        name="attention",
        out_shape=[jax.ShapeDtypeStruct((tokens, width), bf16)] * 2,
        in_specs=[ANY] * 7 + [VMEM],
        out_specs=[VMEM, VMEM],
        scratch_shapes=[
            pltpu.VMEM((tokens, width), bf16),
            pltpu.VMEM((keys, width), bf16),
            pltpu.VMEM((keys, width), bf16),
            pltpu.VMEM((tokens, width), bf16),
            pltpu.VMEM(out_weight.shape, bf16),
            pltpu.VMEM((pairs, tokens, LANES), f32),
            pltpu.VMEM((tokens, LANES), f32),
            pltpu.VMEM((pairs, tokens, LANES), f32),
            pltpu.VMEM((tokens, LANES), f32),
            pltpu.VMEM((tokens, width), bf16),
            pltpu.SemaphoreType.DMA((7,)),
            pltpu.SemaphoreType.DMA((pairs + 1,)),
            pltpu.SemaphoreType.DMA((pairs + 1,)),
        ],
        compiler_params=pltpu.CompilerParams(collective_id=1, has_side_effects=True),
    )(
        query[0], key_cache[0], value_cache[0], key_new[0], value_new[0], resid[0],
        out_weight, ffn_gain[None, :],
    )
    cap = max(2, 3 * tokens // peers)
    slots = cap // 2
    total_rows = peers * slots * width // LANES
    group_tokens = GROUP * slots
    group_rows = group_tokens * width // LANES
    hidden_units = w_gate.shape[2]
    route = routing[0]
    result = pl.pallas_call(
        functools.partial(expert_kernel, peers, cap),
        name="experts",
        out_shape=jax.ShapeDtypeStruct((tokens, width), bf16),
        in_specs=[VMEM] * 5 + [ANY] * 3,
        out_specs=VMEM,
        scratch_shapes=[
            pltpu.VMEM((2, width, hidden_units), bf16),
            pltpu.VMEM((2, width, hidden_units), bf16),
            pltpu.VMEM((2, hidden_units, width), bf16),
            pltpu.VMEM((total_rows, LANES), bf16),
            pltpu.VMEM((total_rows, LANES), bf16),
            pltpu.VMEM((total_rows, LANES), bf16),
            pltpu.VMEM((total_rows, LANES), bf16),
            pltpu.VMEM((group_tokens, width), f32),
            pltpu.VMEM((tokens, width), bf16),
            pltpu.VMEM((tokens, width), bf16),
            pltpu.VMEM((group_rows, group_rows), bf16),
            pltpu.VMEM((group_rows, group_rows), bf16),
            pltpu.SemaphoreType.DMA((3,)),
            pltpu.SemaphoreType.DMA((3,)),
            pltpu.SemaphoreType.DMA((3,)),
            pltpu.SemaphoreType.DMA((peers,)),
            pltpu.SemaphoreType.DMA((peers,)),
            pltpu.SemaphoreType.DMA((peers,)),
            pltpu.SemaphoreType.DMA((peers,)),
            pltpu.SemaphoreType.DMA((2,)),
        ],
        compiler_params=pltpu.CompilerParams(
            collective_id=2, has_side_effects=True, vmem_limit_bytes=50 * 1024 * 1024
        ),
    )(
        normed, hidden, route, route.reshape(1, tokens), router_prob.reshape(tokens, 1),
        w_gate[0], w_up[0], w_down[0],
    )
    return result[None]


def solution(mesh):
    in_specs = (
        P(("groups", "expert"), None, None),
        P(("groups", "expert"), "seq", None),
        P(("groups", "expert"), "seq", None),
        P(("groups", "expert"), None, None),
        P(("groups", "expert"), None, None),
        P(("groups", "expert"), None, None),
        P(("groups", "expert"), None, None),
        P(("groups", "expert"), None),
        P(),
        P(),
        P("expert", None, "seq"),
        P("expert", None, "seq"),
        P("expert", "seq", None),
    )
    out_specs = P(("groups", "expert"), None, None)
    return jax.shard_map(
        functools.partial(on_device, mesh.shape["expert"]),
        mesh=mesh, in_specs=in_specs, out_specs=out_specs, check_vma=False,
    )
```

time: 281 us -> 120 us (0.43)
  blocking collectives: 201 us -> 0 us
  Pallas kernels: 0 us -> 116 us
  starting transfers between devices: 31.7 us -> 0 us
  matrix products: 19 us -> 0 us
  local copies, waits for them, and re-layouts: 19.7 us -> 4.28 us
  other arithmetic: 5.8 us -> 0 us
  waiting for transfers between devices: 2.87 us -> 0 us
    all_to_all x4 -> x0, blocking collectives: 201 us -> none  [the longest x1 118 us: on_device(): lax.all_to_all(outgoing, 'expert', split_axis=0, concat_axis=0, tiled=True)]
    pallas_call x0 -> x2, Pallas kernels: none -> 116 us  [the longest x1 85 us: on_device(): pl.pallas_call(functools.partial(expert_kernel, peers, cap), name='expert...]
    all_to_all x3 -> x0, starting transfers between devices: 31.7 us -> none  [copy_for_each(): return lax.all_to_all(copies, axis, split_axis=0, concat_axis=0, tiled=True)]
    dot_general x11 -> x0, matrix products: 19 us -> none  [the longest x2 3.57 us: partial_attend(): jnp.einsum('qhd,khd->hqk', heads_q, keys_h, preferred_element_type=jnp.fl...]
    unnamed x32 -> x9, local copies, waits for them, and re-layouts: 9.64 us -> 2.61 us
    reduce_sum x3 -> x0, other arithmetic: 4.32 us -> none  [the longest x2 3.02 us: partial_attend(): denom = jnp.sum(expw, axis=2)]
    reshape x3 -> x1, local copies, waits for them, and re-layouts: 4.28 us -> 0.91 us  [on_device(): router_prob.reshape(tokens, 1)]
    all_to_all x3 -> x0, waiting for transfers between devices: 2.87 us -> none  [copy_for_each(): return lax.all_to_all(copies, axis, split_axis=0, concat_axis=0, tiled=True)]
  transfers between devices with their start and end apart: 3 -> 0, of which waited for: 2 -> 0; matrix products, arithmetic and copies ran while one was open for 4% -> 0% of each run, Pallas kernels for 0% -> 0%
where the time goes in v1:
time: 120 us
  Pallas kernels  116 us (97%)
  local copies, waits for them, and re-layouts  4.28 us (4%)
    pallas_call x1, Pallas kernels, on_device(): pl.pallas_call(functools.partial(expert_kernel, peers, cap), name='expert...  85 us
    pallas_call x1, Pallas kernels, on_device(): pl.pallas_call(attention_kernel, name='attention', out_shape=[jax.ShapeDt...  30.9 us
    unnamed x9, local copies, waits for them, and re-layouts  2.61 us

profile of v1, /device:TPU:37, one launch (start us, length us, event | category | flops | bytes accessed | tf_op | source)
XLA Modules:
  0.0 120.2 jit_solution(3706260596001831818)
XLA Ops:
  0.0 0.0 copy-start.3
  0.0 0.0 copy-start
  0.0 0.9 copy.15.prob
  0.9 0.8 copy.14.route_col
  1.7 30.9 %attention.1 = (bf16[128,1024]{1,0:T(8,128)(2,1)}, bf16[128,1024]{1,0:T(8,128)(2,1)}) custom-call(bf16[128,1024]{1,0:T(8,128)(2,1)} %bitcast.22, bf16[384,1024]{1,0:T(8,128)(2,1)} %bitcast.20, bf16[384,1024]{1,0:T(8,128)(2,1)} %bitcast.21, bf16[128,1024]{1,0:T(8,128)(2,1)} %bitcast.23, bf16[128,1024]{1,0:T(8,128)(2,1)} %bitcast.24, ...), custom_call_target="tpu_custom_call" | custom-call | tf_op jit(solution)/shard_map/attention/pallas_call | solution.py:287
  32.6 0.0 copy-done.3
  32.6 0.0 copy-done
  32.6 0.0 copy-start.1
  32.6 0.9 copy-done.1
  33.5 0.0 copy-start.2
  33.5 0.9 copy-done.2
  34.5 85.0 %experts.1 = bf16[128,1024]{1,0:T(8,128)(2,1)S(1)} custom-call(bf16[128,1024]{1,0:T(8,128)(2,1)S(1)} %copy-done.2, bf16[128,1024]{1,0:T(8,128)(2,1)S(1)} %copy-done.1, s32[128,1]{1,0:T(8,128)S(1)} %copy.14.route_col, s32[1,128]{1,0:T(1,128)S(1)} %bitcast.17, f32[128,1]{1,0:T(8,128)S(1)} %copy.15.prob, bf16[1024,1280]{1,0:T(8,128)(2,1)S(1)} %bitcast.14, ...), custom_call_target="tpu_custom_call" | custom-call | tf_op jit(solution)/shard_map/experts/pallas_call | solution.py:320
  119.5 0.7 copy.17
Async XLA Ops:
  0.0 32.6 %copy-start.3 = (s32[1,128,1]{1,2,0:T(1,128)S(1)}, s32[1,128,1]{1,2,0:T(1,128)}, u32[]{:S(2)}) copy-start(s32[1,128,1]{1,2,0:T(1,128)} %param.19) | copy-start | bytes 1540
  0.0 32.6 %copy-start = (bf16[1,1024,1280]{2,1,0:T(8,128)(2,1)S(1)}, bf16[1,1024,1280]{2,1,0:T(8,128)(2,1)}, u32[]{:S(2)}) copy-start(bf16[1,1024,1280]{2,1,0:T(8,128)(2,1)} %param.23) | copy-start | bytes 7864324
  32.6 1.0 copy-start.1
  33.5 0.9 copy-start.2

commit v2 on v1

--- a/solution.py
+++ b/solution.py
@@ -28,9 +28,9 @@
 
 
 def attention_kernel(
-    query, key_cache, value_cache, key_new, value_new, resid, out_weight, gain,
-    hidden_ref, normed_ref,
-    q_v, k_v, v_v, r_v, w_v, sums, stats, sums_in, stats_in, attn,
+    query, key_cache, value_cache, key_new, value_new,
+    attn,
+    q_v, k_v, v_v, sums, stats, sums_in, stats_in,
     copy_sem, send_sem, recv_sem,
 ):
     core = lax.axis_index("seq")
@@ -51,15 +51,13 @@
             (key_new, k_v.at[pl.ds(cached, tokens)]),
             (value_cache, v_v.at[pl.ds(0, cached)]),
             (value_new, v_v.at[pl.ds(cached, tokens)]),
-            (out_weight, w_v),
-            (resid, r_v),
         ])
     ]
     for load in loads:
         load.start()
     stats[...] = jnp.zeros_like(stats)
     pl.semaphore_wait(barrier, 1)
-    for load in loads[:5]:
+    for load in loads:
         load.wait()
 
     def to_other(pair):
@@ -119,26 +117,18 @@
         total = sums[pair] * left + sums_in[pair] * right
         attn[:, pair * LANES : (pair + 1) * LANES] = (total / denom).astype(jnp.bfloat16)
 
-    loads[5].wait()
-    loads[6].wait()
-    hidden = (r_v[...].astype(jnp.float32) + dot(attn[...], w_v[...])).astype(jnp.bfloat16)
-    hidden_ref[...] = hidden
-    hidden_f = hidden.astype(jnp.float32)
-    meansq = jnp.mean(hidden_f * hidden_f, axis=1, keepdims=True)
-    normed_ref[...] = (hidden_f * lax.rsqrt(meansq + 1e-06) * gain[...]).astype(jnp.bfloat16)
-
 
 def expert_kernel(
     peers, cap,
-    normed, hidden, route_col, route_row, prob, w_gate, w_up, w_down,
+    attn, resid, route_row, prob_row, gain, w_out, w_gate, w_up, w_down,
     out,
-    wg, wu, wd, outgoing, arrived, results, returned, total, part, part_in, shuffle, shuffle_t,
+    wo, wg, wu, wd, outgoing, arrived, results, returned, total, part, part_in, shuffle, shuffle_t,
     copy_sem, wsend_sem, wrecv_sem, send_sem, recv_sem, back_send, back_recv, last_sem,
 ):
     me = lax.axis_index("expert")
     core = lax.axis_index("seq")
     other = {"seq": 1 - core}
-    tokens, width = normed.shape
+    tokens, width = attn.shape
     blocks = width // LANES
     slots = cap // 2
     rows = slots * blocks
@@ -146,29 +136,42 @@
     group_rows = GROUP * rows
     groups = peers // GROUP
     half = peers // 2
-    rels = [half + ((n + 1) // 2) * (1 - 2 * (n % 2)) for n in range(peers)]
+
+    def ahead(rel):
+        return {"expert": lax.rem(me + rel, peers)}
 
     barrier = pltpu.get_barrier_semaphore()
-    for rel in rels[:-1]:
-        pl.semaphore_signal(barrier, inc=1, device_id={"expert": lax.rem(me + rel, peers)}, device_id_type=MESH)
     pl.semaphore_signal(barrier, inc=1, device_id=other, device_id_type=MESH)
+    for rel in range(1, peers):
+        pl.semaphore_signal(barrier, inc=1, device_id=ahead(rel), device_id_type=MESH)
     loads = [
-        pltpu.make_async_copy(src, dst.at[0], copy_sem.at[i])
-        for i, (src, dst) in enumerate([(w_gate, wg), (w_up, wu), (w_down, wd)])
+        pltpu.make_async_copy(src, dst, copy_sem.at[i])
+        for i, (src, dst) in enumerate([
+            (w_out, wo), (w_gate, wg.at[0]), (w_up, wu.at[0]), (w_down, wd.at[0]),
+        ])
     ]
     for load in loads:
         load.start()
 
-    same = route_col[...] == route_row[...]
+    def place_of(rel):
+        if isinstance(rel, int):
+            return 2 * (rel - half) if rel > half else max(2 * (half - rel) - 1, 0)
+        return jnp.where(rel > half, 2 * (rel - half), jnp.maximum(2 * (half - rel) - 1, 0))
+
     first, second = iota((tokens, tokens), 0), iota((tokens, tokens), 1)
 
+    def column(row):
+        return jnp.sum(jnp.where(first == second, row, jnp.zeros_like(row)), axis=1, keepdims=True)
+
+    route_col = column(route_row[...])
+    same = route_col == route_row[...]
+
     def place(route, rank):
-        delta = lax.rem(route - me + peers, peers) - half
-        order = jnp.where(delta > 0, 2 * delta, jnp.maximum(-2 * delta - 1, 0))
+        order = place_of(lax.rem(route - me + peers, peers))
         slot = rank - core * slots
         return jnp.where((slot >= 0) & (slot < slots), order * slots + slot, -1)
 
-    place_col = place(route_col[...], jnp.sum(jnp.where(same & (second < first), 1, 0), axis=1, keepdims=True))
+    place_col = place(route_col, jnp.sum(jnp.where(same & (second < first), 1, 0), axis=1, keepdims=True))
     place_row = place(route_row[...], jnp.sum(jnp.where(same & (first < second), 1, 0), axis=0, keepdims=True))
 
     def moves(packed, plain):
@@ -189,24 +192,42 @@
             [plain[j * group_tokens : (j + 1) * group_tokens] for j in range(blocks)], axis=1
         )
 
+    loads[0].wait()
+    hidden = (resid[...].astype(jnp.float32) + dot(attn[...], wo[...])).astype(jnp.bfloat16)
+    hidden_f = hidden.astype(jnp.float32)
+    meansq = jnp.mean(hidden_f * hidden_f, axis=1, keepdims=True)
+    normed = (hidden_f * lax.rsqrt(meansq + 1e-06) * gain[...]).astype(jnp.bfloat16)
+
     for g in range(groups):
         picked = jnp.where(
             place_row == g * group_tokens + iota((group_tokens, tokens), 0), 1.0, 0.0
         ).astype(jnp.bfloat16)
-        chosen = dot(picked, normed[...]).astype(jnp.bfloat16)
+        chosen = dot(picked, normed).astype(jnp.bfloat16)
         outgoing[pl.ds(g * group_rows, group_rows)] = pack(chosen)
-    own = pl.ds((peers - 1) * rows, rows)
+    own_place = place_of(0)
+    own = pl.ds(own_place * rows, rows)
     arrived[own] = outgoing[own]
 
+    def sent(rel):
+        n = place_of(rel)
+        spot = pl.ds(n * rows, rows)
+        return pltpu.make_async_remote_copy(
+            src_ref=outgoing.at[spot], dst_ref=arrived.at[spot], send_sem=send_sem.at[n], recv_sem=recv_sem.at[n],
+            device_id=ahead(rel), device_id_type=MESH,
+        )
+
+    def answered(rel):
+        n = place_of(rel)
+        spot = pl.ds(n * rows, rows)
+        return pltpu.make_async_remote_copy(
+            src_ref=results.at[spot], dst_ref=returned.at[spot], send_sem=back_send.at[n], recv_sem=back_recv.at[n],
+            device_id=ahead(peers - rel), device_id_type=MESH,
+        )
+
     pl.semaphore_wait(barrier, peers)
-    sends = []
-    for n in range(peers - 1):
-        spot = pl.ds(n * rows, rows)
-        sends.append(pltpu.make_async_remote_copy(
-            src_ref=outgoing.at[spot], dst_ref=arrived.at[spot], send_sem=send_sem.at[n], recv_sem=recv_sem.at[n],
-            device_id={"expert": lax.rem(me + rels[n], peers)}, device_id_type=MESH,
-        ))
-        sends[-1].start()
+    by_place = sorted(range(1, peers), key=place_of)
+    for rel in by_place:
+        sent(rel).start()
     halves = [
         pltpu.make_async_remote_copy(
             src_ref=src, dst_ref=dst.at[1], send_sem=wsend_sem.at[i], recv_sem=wrecv_sem.at[i],
@@ -216,17 +237,20 @@
     ]
     for copy in halves:
         copy.start()
-    for load in loads:
+    for load in loads[1:]:
         load.wait()
     for copy in halves:
         copy.wait_recv()
 
+    members = [[] for _ in range(groups)]
+    for rel in by_place:
+        members[place_of(rel) // GROUP].append(rel)
+
     chunk = 2 * LANES
     chunks = wg.shape[2] // chunk
-    backs = []
     for g in range(groups):
-        for n in range(g * GROUP, min((g + 1) * GROUP, peers - 1)):
-            sends[n].wait_recv()
+        for rel in members[g]:
+            sent(rel).wait_recv()
         rows_in = unpack(arrived[pl.ds(g * group_rows, group_rows)])
         total[...] = jnp.zeros_like(total)
 
@@ -240,19 +264,14 @@
 
         lax.fori_loop(0, 2 * chunks, step, 0)
         results[pl.ds(g * group_rows, group_rows)] = pack(total[...].astype(jnp.bfloat16))
-        for n in range(g * GROUP, min((g + 1) * GROUP, peers - 1)):
-            spot = pl.ds(n * rows, rows)
-            backs.append(pltpu.make_async_remote_copy(
-                src_ref=results.at[spot], dst_ref=returned.at[spot], send_sem=back_send.at[n], recv_sem=back_recv.at[n],
-                device_id={"expert": lax.rem(me + peers - rels[n], peers)}, device_id_type=MESH,
-            ))
-            backs[-1].start()
+        for rel in members[g]:
+            answered(rel).start()
     returned[own] = results[own]
 
     summed = jnp.zeros((tokens, width), jnp.float32)
     for g in range(groups):
-        for n in range(g * GROUP, min((g + 1) * GROUP, peers - 1)):
-            backs[n].wait_recv()
+        for rel in members[g]:
+            answered(rel).wait_recv()
         rows_back = unpack(returned[pl.ds(g * group_rows, group_rows)])
         picked = jnp.where(
             place_col == g * group_tokens + iota((tokens, group_tokens), 1), 1.0, 0.0
@@ -266,8 +285,11 @@
     last.start()
     last.wait_recv()
     expert_out = summed + part_in[...].astype(jnp.float32)
-    out[...] = (hidden[...].astype(jnp.float32) + prob[...] * expert_out).astype(jnp.bfloat16)
-    for copy in sends + halves + backs + [last]:
+    out[...] = (hidden.astype(jnp.float32) + column(prob_row[...]) * expert_out).astype(jnp.bfloat16)
+    for rel in range(1, peers):
+        sent(rel).wait_send()
+        answered(rel).wait_send()
+    for copy in halves + [last]:
         copy.wait_send()
 
 
@@ -284,46 +306,40 @@
     keys = cached + tokens
     pairs = width // LANES
     bf16, f32 = jnp.bfloat16, jnp.float32
-    hidden, normed = pl.pallas_call(
+    attn = pl.pallas_call(
         attention_kernel,
         name="attention",
-        out_shape=[jax.ShapeDtypeStruct((tokens, width), bf16)] * 2,
-        in_specs=[ANY] * 7 + [VMEM],
-        out_specs=[VMEM, VMEM],
+        out_shape=jax.ShapeDtypeStruct((tokens, width), bf16),
+        in_specs=[ANY] * 5,
+        out_specs=VMEM,
         scratch_shapes=[
             pltpu.VMEM((tokens, width), bf16),
             pltpu.VMEM((keys, width), bf16),
             pltpu.VMEM((keys, width), bf16),
-            pltpu.VMEM((tokens, width), bf16),
-            pltpu.VMEM(out_weight.shape, bf16),
             pltpu.VMEM((pairs, tokens, LANES), f32),
             pltpu.VMEM((tokens, LANES), f32),
             pltpu.VMEM((pairs, tokens, LANES), f32),
             pltpu.VMEM((tokens, LANES), f32),
-            pltpu.VMEM((tokens, width), bf16),
-            pltpu.SemaphoreType.DMA((7,)),
+            pltpu.SemaphoreType.DMA((5,)),
             pltpu.SemaphoreType.DMA((pairs + 1,)),
             pltpu.SemaphoreType.DMA((pairs + 1,)),
         ],
         compiler_params=pltpu.CompilerParams(collective_id=1, has_side_effects=True),
-    )(
-        query[0], key_cache[0], value_cache[0], key_new[0], value_new[0], resid[0],
-        out_weight, ffn_gain[None, :],
-    )
+    )(query[0], key_cache[0], value_cache[0], key_new[0], value_new[0])
     cap = max(2, 3 * tokens // peers)
     slots = cap // 2
     total_rows = peers * slots * width // LANES
     group_tokens = GROUP * slots
     group_rows = group_tokens * width // LANES
     hidden_units = w_gate.shape[2]
-    route = routing[0]
     result = pl.pallas_call(
         functools.partial(expert_kernel, peers, cap),
         name="experts",
         out_shape=jax.ShapeDtypeStruct((tokens, width), bf16),
-        in_specs=[VMEM] * 5 + [ANY] * 3,
+        in_specs=[VMEM] * 5 + [ANY] * 4,
         out_specs=VMEM,
         scratch_shapes=[
+            pltpu.VMEM(out_weight.shape, bf16),
             pltpu.VMEM((2, width, hidden_units), bf16),
             pltpu.VMEM((2, width, hidden_units), bf16),
             pltpu.VMEM((2, hidden_units, width), bf16),
@@ -336,7 +352,7 @@
             pltpu.VMEM((tokens, width), bf16),
             pltpu.VMEM((group_rows, group_rows), bf16),
             pltpu.VMEM((group_rows, group_rows), bf16),
-            pltpu.SemaphoreType.DMA((3,)),
+            pltpu.SemaphoreType.DMA((4,)),
             pltpu.SemaphoreType.DMA((3,)),
             pltpu.SemaphoreType.DMA((3,)),
             pltpu.SemaphoreType.DMA((peers,)),
@@ -349,8 +365,8 @@
             collective_id=2, has_side_effects=True, vmem_limit_bytes=50 * 1024 * 1024
         ),
     )(
-        normed, hidden, route, route.reshape(1, tokens), router_prob.reshape(tokens, 1),
-        w_gate[0], w_up[0], w_down[0],
+        attn, resid[0], routing.reshape(1, tokens), router_prob, ffn_gain[None, :],
+        out_weight, w_gate[0], w_up[0], w_down[0],
     )
     return result[None]
 

time: 120 us -> 117 us (0.975)
  local copies, waits for them, and re-layouts: 4.28 us -> 1.67 us
    unnamed x9 -> x13, local copies, waits for them, and re-layouts: 2.61 us -> 1.67 us
where the time goes in v2:
time: 117 us
  Pallas kernels  115 us (98%)
  local copies, waits for them, and re-layouts  1.67 us (1%)
    pallas_call x1, Pallas kernels, on_device(): pl.pallas_call(functools.partial(expert_kernel, peers, cap), name='expert...  85.3 us
    pallas_call x1, Pallas kernels, on_device(): pl.pallas_call(attention_kernel, name='attention', out_shape=jax.ShapeDty...  29.7 us

profile of v2, /device:TPU:37, one launch (start us, length us, event | category | flops | bytes accessed | tf_op | source)
XLA Modules:
  0.0 116.8 jit_solution(9462540791630327826)
XLA Ops:
  0.0 0.0 copy-start.3
  0.0 0.0 copy-start
  0.0 0.0 copy-start.5
  0.0 0.0 copy-start.4
  0.0 0.0 copy-start.2
  0.0 29.7 %attention.1.attn = bf16[128,1024]{1,0:T(8,128)(2,1)} custom-call(bf16[128,1024]{1,0:T(8,128)(2,1)} %bitcast.21, bf16[384,1024]{1,0:T(8,128)(2,1)} %bitcast.19, bf16[384,1024]{1,0:T(8,128)(2,1)} %bitcast.20, bf16[128,1024]{1,0:T(8,128)(2,1)} %bitcast.22, bf16[128,1024]{1,0:T(8,128)(2,1)} %bitcast.23), custom_call_target="tpu_custom_call" | custom-call | tf_op jit(solution)/shard_map/attention/pallas_call | solution.py:309
  29.7 0.0 copy-done.3
  29.8 0.0 copy-done
  29.8 0.0 copy-done.5
  29.8 0.0 copy-done.4
  29.8 0.0 copy-done.2
  29.8 0.0 copy-start.1
  29.8 0.9 copy-done.1
  30.8 85.3 %experts.1 = bf16[128,1024]{1,0:T(8,128)(2,1)S(1)} custom-call(bf16[128,1024]{1,0:T(8,128)(2,1)S(1)} %copy-done.1, bf16[128,1024]{1,0:T(8,128)(2,1)S(1)} %bitcast.13, s32[1,128]{1,0:T(1,128)S(1)} %bitcast.15, f32[1,128]{1,0:T(1,128)S(1)} %copy-done.5, f32[1,1024]{1,0:T(1,128)S(1)} %bitcast.14, bf16[1024,1024]{1,0:T(8,128)(2,1)S(1)} %copy-done, ...), custom_call_target="tpu_custom_call" | custom-call | tf_op jit(solution)/shard_map/experts/pallas_call | solution.py:335
  116.0 0.7 copy.15
Async XLA Ops:
  0.0 29.8 %copy-start.3 = (f32[1024]{0:T(1024)S(1)}, f32[1024]{0:T(1024)}, u32[]{:S(2)}) copy-start(f32[1024]{0:T(1024)} %param.22) | copy-start | bytes 12292
  0.0 29.8 %copy-start = (bf16[1024,1024]{1,0:T(8,128)(2,1)S(1)}, bf16[1024,1024]{1,0:T(8,128)(2,1)}, u32[]{:S(2)}) copy-start(bf16[1024,1024]{1,0:T(8,128)(2,1)} %w_out.1) | copy-start | bytes 6291460
  0.0 29.8 %copy-start.5 = (f32[1,128]{1,0:T(1,128)S(1)}, f32[1,128]{1,0:T(1,128)}, u32[]{:S(2)}) copy-start(f32[1,128]{1,0:T(1,128)} %prob_row.1) | copy-start | bytes 1540
  0.0 29.8 %copy-start.4 = (s32[1,128,1]{1,2,0:T(1,128)S(1)}, s32[1,128,1]{1,2,0:T(1,128)}, u32[]{:S(2)}) copy-start(s32[1,128,1]{1,2,0:T(1,128)} %param.19) | copy-start | bytes 1540
  0.0 29.8 %copy-start.2 = (bf16[1,128,1024]{2,1,0:T(8,128)(2,1)S(1)}, bf16[1,128,1024]{2,1,0:T(8,128)(2,1)}, u32[]{:S(2)}) copy-start(bf16[1,128,1024]{2,1,0:T(8,128)(2,1)} %param.18) | copy-start | bytes 786436
  29.8 1.0 copy-start.1

commit v3 on v2

--- a/solution.py
+++ b/solution.py
@@ -13,6 +13,7 @@
 GROUP = 8
 MESH = pl.DeviceIdType.MESH
 NEG = -1e30
+VMEM_GRANT = 50 * 1024 * 1024
 
 
 def iota(shape, dim):
@@ -30,99 +31,89 @@
 def attention_kernel(
     query, key_cache, value_cache, key_new, value_new,
     attn,
-    q_v, k_v, v_v, sums, stats, sums_in, stats_in,
+    q_v, kc_v, vc_v, kn_v, vn_v, parts, parts_in,
     copy_sem, send_sem, recv_sem,
 ):
     core = lax.axis_index("seq")
     other = {"seq": 1 - core}
     tokens, width = q_v.shape
-    cached = key_cache.shape[0]
-    keys = k_v.shape[0]
     pairs = width // LANES
     fresh_half = tokens // 2
+    pieces = 2
+    span = width // pieces
 
     barrier = pltpu.get_barrier_semaphore()
     pl.semaphore_signal(barrier, inc=1, device_id=other, device_id_type=MESH)
+    arrays = [(query, q_v), (key_cache, kc_v), (key_new, kn_v), (value_cache, vc_v), (value_new, vn_v)]
     loads = [
-        pltpu.make_async_copy(src, dst, copy_sem.at[i])
-        for i, (src, dst) in enumerate([
-            (query, q_v),
-            (key_cache, k_v.at[pl.ds(0, cached)]),
-            (key_new, k_v.at[pl.ds(cached, tokens)]),
-            (value_cache, v_v.at[pl.ds(0, cached)]),
-            (value_new, v_v.at[pl.ds(cached, tokens)]),
-        ])
+        [
+            pltpu.make_async_copy(
+                src.at[:, pl.ds(piece * span, span)], dst.at[:, pl.ds(piece * span, span)], copy_sem.at[piece, i]
+            )
+            for i, (src, dst) in enumerate(arrays)
+        ]
+        for piece in range(pieces)
     ]
-    for load in loads:
-        load.start()
-    stats[...] = jnp.zeros_like(stats)
-    pl.semaphore_wait(barrier, 1)
-    for load in loads:
-        load.wait()
+    for piece in loads:
+        for load in piece:
+            load.start()
 
     def to_other(pair):
         return pltpu.make_async_remote_copy(
-            src_ref=sums.at[pair], dst_ref=sums_in.at[pair],
+            src_ref=parts.at[pair], dst_ref=parts_in.at[pair],
             send_sem=send_sem.at[pair], recv_sem=recv_sem.at[pair],
             device_id=other, device_id_type=MESH,
         )
 
     low = iota((tokens, LANES), 1) < HEAD_DIM
-    lane = iota((tokens, LANES), 1)
-    col = iota((2 * tokens, keys), 1) - cached
-    row = lax.rem(iota((2 * tokens, keys), 0), tokens)
-    mine = lax.div(jnp.maximum(col, 0), fresh_half) == core
-    allowed = (col < 0) | ((col <= row) & mine)
+    col = iota((2 * tokens, tokens), 1)
+    row = lax.rem(iota((2 * tokens, tokens), 0), tokens)
+    allowed = (col <= row) & (lax.div(col, fresh_half) == core)
+    pl.semaphore_wait(barrier, 1)
+
+    def sides(values):
+        return jnp.where(low, values[:tokens], values[tokens:])
 
     def one_pair(pair, carry):
         lanes = pl.ds(pl.multiple_of(pair * LANES, LANES), LANES)
         q = q_v[:, lanes] * jnp.bfloat16(1.0 / math.sqrt(HEAD_DIM))
         zero = jnp.zeros_like(q)
         both = jnp.concatenate([jnp.where(low, q, zero), jnp.where(low, zero, q)], axis=0)
-        scores = jnp.where(allowed, dot_t(both, k_v[:, lanes]), NEG)
-        peak = jnp.max(scores, axis=1, keepdims=True)
-        expw = jnp.exp(scores - peak)
-        denom = jnp.sum(expw, axis=1, keepdims=True)
-        weighted = dot(expw.astype(jnp.bfloat16), v_v[:, lanes])
-        sums[pair] = jnp.where(low, weighted[:tokens], weighted[tokens:])
-        kept = stats[...]
-        for side in range(2):
-            rows = slice(side * tokens, (side + 1) * tokens)
-            head = 2 * pair + side
-            kept = jnp.where(lane == head, peak[rows], kept)
-            kept = jnp.where(lane == head + 2 * pairs, denom[rows], kept)
-        stats[...] = kept
+        old = dot_t(both, kc_v[:, lanes])
+        new = jnp.where(allowed, dot_t(both, kn_v[:, lanes]), NEG)
+        peak = jnp.maximum(jnp.max(old, axis=1, keepdims=True), jnp.max(new, axis=1, keepdims=True))
+        exp_old, exp_new = jnp.exp(old - peak), jnp.exp(new - peak)
+        denom = jnp.sum(exp_old, axis=1, keepdims=True) + jnp.sum(exp_new, axis=1, keepdims=True)
+        weighted = dot(exp_old.astype(jnp.bfloat16), vc_v[:, lanes]) + dot(exp_new.astype(jnp.bfloat16), vn_v[:, lanes])
+        spread = (2 * tokens, LANES)
+        parts[pair, 0] = sides(weighted)
+        parts[pair, 1] = sides(jnp.broadcast_to(peak, spread))
+        parts[pair, 2] = sides(jnp.broadcast_to(denom, spread))
         to_other(pair).start()
         return carry
 
-    lax.fori_loop(0, pairs, one_pair, 0)
-    stat_copy = pltpu.make_async_remote_copy(
-        src_ref=stats, dst_ref=stats_in, send_sem=send_sem.at[pairs], recv_sem=recv_sem.at[pairs],
-        device_id=other, device_id_type=MESH,
-    )
-    stat_copy.start()
-    stat_copy.wait()
-
-    for pair in range(pairs):
+    def merge(pair, carry):
         to_other(pair).wait()
-        own, their = stats[...], stats_in[...]
-        spread = []
-        for kind in (own, their):
-            for offset in (0, 2 * pairs):
-                spots = [kind[:, offset + 2 * pair + side : offset + 2 * pair + side + 1] for side in range(2)]
-                spread.append(jnp.where(low, spots[0], spots[1]))
-        peak = jnp.maximum(spread[0], spread[2])
-        left, right = jnp.exp(spread[0] - peak), jnp.exp(spread[2] - peak)
-        denom = spread[1] * left + spread[3] * right
-        total = sums[pair] * left + sums_in[pair] * right
-        attn[:, pair * LANES : (pair + 1) * LANES] = (total / denom).astype(jnp.bfloat16)
+        peak = jnp.maximum(parts[pair, 1], parts_in[pair, 1])
+        left, right = jnp.exp(parts[pair, 1] - peak), jnp.exp(parts_in[pair, 1] - peak)
+        denom = parts[pair, 2] * left + parts_in[pair, 2] * right
+        total = parts[pair, 0] * left + parts_in[pair, 0] * right
+        attn[:, pl.ds(pl.multiple_of(pair * LANES, LANES), LANES)] = (total / denom).astype(jnp.bfloat16)
+        return carry
+
+    each = pairs // pieces
+    for piece in range(pieces):
+        for load in loads[piece]:
+            load.wait()
+        lax.fori_loop(piece * each, (piece + 1) * each, one_pair, 0)
+    lax.fori_loop(0, pairs, merge, 0)
 
 
 def expert_kernel(
     peers, cap,
     attn, resid, route_row, prob_row, gain, w_out, w_gate, w_up, w_down,
     out,
-    wo, wg, wu, wd, outgoing, arrived, results, returned, total, part, part_in, shuffle, shuffle_t,
+    wg, wu, wd, outgoing, arrived, results, returned, total, part, part_in, shuffle, shuffle_t,
     copy_sem, wsend_sem, wrecv_sem, send_sem, recv_sem, back_send, back_recv, last_sem,
 ):
     me = lax.axis_index("expert")
@@ -147,7 +138,7 @@
     loads = [
         pltpu.make_async_copy(src, dst, copy_sem.at[i])
         for i, (src, dst) in enumerate([
-            (w_out, wo), (w_gate, wg.at[0]), (w_up, wu.at[0]), (w_down, wd.at[0]),
+            (w_gate, wg.at[0]), (w_up, wu.at[0]), (w_down, wd.at[0]),
         ])
     ]
     for load in loads:
@@ -192,8 +183,7 @@
             [plain[j * group_tokens : (j + 1) * group_tokens] for j in range(blocks)], axis=1
         )
 
-    loads[0].wait()
-    hidden = (resid[...].astype(jnp.float32) + dot(attn[...], wo[...])).astype(jnp.bfloat16)
+    hidden = (resid[...].astype(jnp.float32) + dot(attn[...], w_out[...])).astype(jnp.bfloat16)
     hidden_f = hidden.astype(jnp.float32)
     meansq = jnp.mean(hidden_f * hidden_f, axis=1, keepdims=True)
     normed = (hidden_f * lax.rsqrt(meansq + 1e-06) * gain[...]).astype(jnp.bfloat16)
@@ -237,7 +227,7 @@
     ]
     for copy in halves:
         copy.start()
-    for load in loads[1:]:
+    for load in loads:
         load.wait()
     for copy in halves:
         copy.wait_recv()
@@ -303,7 +293,6 @@
 ):
     tokens, width = query.shape[1:]
     cached = key_cache.shape[1]
-    keys = cached + tokens
     pairs = width // LANES
     bf16, f32 = jnp.bfloat16, jnp.float32
     attn = pl.pallas_call(
@@ -314,15 +303,15 @@
         out_specs=VMEM,
         scratch_shapes=[
             pltpu.VMEM((tokens, width), bf16),
-            pltpu.VMEM((keys, width), bf16),
-            pltpu.VMEM((keys, width), bf16),
-            pltpu.VMEM((pairs, tokens, LANES), f32),
-            pltpu.VMEM((tokens, LANES), f32),
-            pltpu.VMEM((pairs, tokens, LANES), f32),
-            pltpu.VMEM((tokens, LANES), f32),
-            pltpu.SemaphoreType.DMA((5,)),
-            pltpu.SemaphoreType.DMA((pairs + 1,)),
-            pltpu.SemaphoreType.DMA((pairs + 1,)),
+            pltpu.VMEM((cached, width), bf16),
+            pltpu.VMEM((cached, width), bf16),
+            pltpu.VMEM((tokens, width), bf16),
+            pltpu.VMEM((tokens, width), bf16),
+            pltpu.VMEM((pairs, 3, tokens, LANES), f32),
+            pltpu.VMEM((pairs, 3, tokens, LANES), f32),
+            pltpu.SemaphoreType.DMA((2, 5)),
+            pltpu.SemaphoreType.DMA((pairs,)),
+            pltpu.SemaphoreType.DMA((pairs,)),
         ],
         compiler_params=pltpu.CompilerParams(collective_id=1, has_side_effects=True),
     )(query[0], key_cache[0], value_cache[0], key_new[0], value_new[0])
@@ -336,10 +325,9 @@
         functools.partial(expert_kernel, peers, cap),
         name="experts",
         out_shape=jax.ShapeDtypeStruct((tokens, width), bf16),
-        in_specs=[VMEM] * 5 + [ANY] * 4,
+        in_specs=[VMEM] * 6 + [ANY] * 3,
         out_specs=VMEM,
         scratch_shapes=[
-            pltpu.VMEM(out_weight.shape, bf16),
             pltpu.VMEM((2, width, hidden_units), bf16),
             pltpu.VMEM((2, width, hidden_units), bf16),
             pltpu.VMEM((2, hidden_units, width), bf16),
@@ -352,7 +340,7 @@
             pltpu.VMEM((tokens, width), bf16),
             pltpu.VMEM((group_rows, group_rows), bf16),
             pltpu.VMEM((group_rows, group_rows), bf16),
-            pltpu.SemaphoreType.DMA((4,)),
+            pltpu.SemaphoreType.DMA((3,)),
             pltpu.SemaphoreType.DMA((3,)),
             pltpu.SemaphoreType.DMA((3,)),
             pltpu.SemaphoreType.DMA((peers,)),
@@ -362,7 +350,7 @@
             pltpu.SemaphoreType.DMA((2,)),
         ],
         compiler_params=pltpu.CompilerParams(
-            collective_id=2, has_side_effects=True, vmem_limit_bytes=50 * 1024 * 1024
+            collective_id=2, has_side_effects=True, vmem_limit_bytes=VMEM_GRANT
         ),
     )(
         attn, resid[0], routing.reshape(1, tokens), router_prob, ffn_gain[None, :],

time: 117 us -> 115 us (0.983)
  Pallas kernels: 115 us -> 113 us
    pallas_call x1, Pallas kernels: 29.7 us -> 28.1 us  [on_device(): pl.pallas_call(attention_kernel, name='attention', out_shape=jax.ShapeDty...]
where the time goes in v3:
time: 115 us
  Pallas kernels  113 us (98%)
  local copies, waits for them, and re-layouts  1.67 us (1%)
    pallas_call x1, Pallas kernels, on_device(): pl.pallas_call(functools.partial(expert_kernel, peers, cap), name='expert...  85.3 us
    pallas_call x1, Pallas kernels, on_device(): pl.pallas_call(attention_kernel, name='attention', out_shape=jax.ShapeDty...  28.1 us

profile of v3, /device:TPU:37, one launch (start us, length us, event | category | flops | bytes accessed | tf_op | source)
XLA Modules:
  0.0 115.2 jit_solution(10916704755727010676)
XLA Ops:
  0.0 0.0 copy-start.3
  0.0 0.0 copy-start
  0.0 0.0 copy-start.5
  0.0 0.0 copy-start.4
  0.0 0.0 copy-start.2
  0.0 28.1 %attention.1.attn = bf16[128,1024]{1,0:T(8,128)(2,1)} custom-call(bf16[128,1024]{1,0:T(8,128)(2,1)} %bitcast.21, bf16[384,1024]{1,0:T(8,128)(2,1)} %bitcast.19, bf16[384,1024]{1,0:T(8,128)(2,1)} %bitcast.20, bf16[128,1024]{1,0:T(8,128)(2,1)} %bitcast.22, bf16[128,1024]{1,0:T(8,128)(2,1)} %bitcast.23), custom_call_target="tpu_custom_call" | custom-call | tf_op jit(solution)/shard_map/attention/pallas_call | solution.py:298
  28.2 0.0 copy-done.3
  28.2 0.0 copy-done
  28.2 0.0 copy-done.5
  28.2 0.0 copy-done.4
  28.2 0.0 copy-done.2
  28.2 0.0 copy-start.1
  28.2 0.9 copy-done.1
  29.2 85.3 %experts.1 = bf16[128,1024]{1,0:T(8,128)(2,1)S(1)} custom-call(bf16[128,1024]{1,0:T(8,128)(2,1)S(1)} %copy-done.1, bf16[128,1024]{1,0:T(8,128)(2,1)S(1)} %bitcast.13, s32[1,128]{1,0:T(1,128)S(1)} %bitcast.15, f32[1,128]{1,0:T(1,128)S(1)} %copy-done.5, f32[1,1024]{1,0:T(1,128)S(1)} %bitcast.14, bf16[1024,1024]{1,0:T(8,128)(2,1)S(1)} %copy-done, ...), custom_call_target="tpu_custom_call" | custom-call | tf_op jit(solution)/shard_map/experts/pallas_call | solution.py:324
  114.5 0.7 copy.15
Async XLA Ops:
  0.0 28.2 %copy-start.3 = (f32[1024]{0:T(1024)S(1)}, f32[1024]{0:T(1024)}, u32[]{:S(2)}) copy-start(f32[1024]{0:T(1024)} %param.22) | copy-start | bytes 12292
  0.0 28.2 %copy-start = (bf16[1024,1024]{1,0:T(8,128)(2,1)S(1)}, bf16[1024,1024]{1,0:T(8,128)(2,1)}, u32[]{:S(2)}) copy-start(bf16[1024,1024]{1,0:T(8,128)(2,1)} %w_out.1) | copy-start | bytes 6291460
  0.0 28.2 %copy-start.5 = (f32[1,128]{1,0:T(1,128)S(1)}, f32[1,128]{1,0:T(1,128)}, u32[]{:S(2)}) copy-start(f32[1,128]{1,0:T(1,128)} %prob_row.1) | copy-start | bytes 1540
  0.0 28.2 %copy-start.4 = (s32[1,128,1]{1,2,0:T(1,128)S(1)}, s32[1,128,1]{1,2,0:T(1,128)}, u32[]{:S(2)}) copy-start(s32[1,128,1]{1,2,0:T(1,128)} %param.19) | copy-start | bytes 1540
  0.0 28.2 %copy-start.2 = (bf16[1,128,1024]{2,1,0:T(8,128)(2,1)S(1)}, bf16[1,128,1024]{2,1,0:T(8,128)(2,1)}, u32[]{:S(2)}) copy-start(bf16[1,128,1024]{2,1,0:T(8,128)(2,1)} %param.18) | copy-start | bytes 786436
  28.2 1.0 copy-start.1

commit v4 on v3

--- a/solution.py
+++ b/solution.py
@@ -13,7 +13,7 @@
 GROUP = 8
 MESH = pl.DeviceIdType.MESH
 NEG = -1e30
-VMEM_GRANT = 50 * 1024 * 1024
+VMEM_GRANT = 66_600_000
 
 
 def iota(shape, dim):
@@ -28,40 +28,68 @@
     return lax.dot_general(a, b, (((1,), (1,)), ((), ())), preferred_element_type=jnp.float32)
 
 
-def attention_kernel(
+def expert_kernel(
+    peers, cap,
     query, key_cache, value_cache, key_new, value_new,
-    attn,
-    q_v, kc_v, vc_v, kn_v, vn_v, parts, parts_in,
-    copy_sem, send_sem, recv_sem,
+    resid_in, route_in, prob_in, gain_in, w_out_in, w_gate, w_up, w_down,
+    out,
+    resid, route_row, prob_row, gain, w_out, small_sem, q_v, kc_v, vc_v, kn_v, vn_v, parts, parts_in, attn, early_sem, part_send, part_recv,
+    wg, wu, wd, outgoing, arrived, results, returned, total, part, part_in, shuffle, shuffle_t,
+    copy_sem, wsend_sem, wrecv_sem, send_sem, recv_sem, back_send, back_recv, last_sem,
 ):
+    me = lax.axis_index("expert")
     core = lax.axis_index("seq")
     other = {"seq": 1 - core}
     tokens, width = q_v.shape
+    blocks = width // LANES
+    slots = cap // 2
+    rows = slots * blocks
+    group_tokens = GROUP * slots
+    group_rows = GROUP * rows
+    groups = peers // GROUP
+    half = peers // 2
+
+    def ahead(rel):
+        return {"expert": lax.rem(me + rel, peers)}
+
+    barrier = pltpu.get_barrier_semaphore()
+    pl.semaphore_signal(barrier, inc=1, device_id=other, device_id_type=MESH)
+    for rel in range(1, peers):
+        pl.semaphore_signal(barrier, inc=1, device_id=ahead(rel), device_id_type=MESH)
+    loads = [
+        pltpu.make_async_copy(src, dst, copy_sem.at[i])
+        for i, (src, dst) in enumerate([
+            (w_gate, wg.at[0]), (w_up, wu.at[0]), (w_down, wd.at[0]),
+        ])
+    ]
     pairs = width // LANES
     fresh_half = tokens // 2
     pieces = 2
     span = width // pieces
-
-    barrier = pltpu.get_barrier_semaphore()
-    pl.semaphore_signal(barrier, inc=1, device_id=other, device_id_type=MESH)
     arrays = [(query, q_v), (key_cache, kc_v), (key_new, kn_v), (value_cache, vc_v), (value_new, vn_v)]
-    loads = [
+    early = [
         [
             pltpu.make_async_copy(
-                src.at[:, pl.ds(piece * span, span)], dst.at[:, pl.ds(piece * span, span)], copy_sem.at[piece, i]
+                src.at[:, pl.ds(piece * span, span)], dst.at[:, pl.ds(piece * span, span)], early_sem.at[piece, i]
             )
             for i, (src, dst) in enumerate(arrays)
         ]
         for piece in range(pieces)
     ]
-    for piece in loads:
+    small = [
+        pltpu.make_async_copy(src, dst, small_sem.at[i])
+        for i, (src, dst) in enumerate([
+            (route_in, route_row), (prob_in, prob_row), (gain_in, gain), (resid_in, resid), (w_out_in, w_out),
+        ])
+    ]
+    for piece in early + [small]:
         for load in piece:
             load.start()
 
     def to_other(pair):
         return pltpu.make_async_remote_copy(
             src_ref=parts.at[pair], dst_ref=parts_in.at[pair],
-            send_sem=send_sem.at[pair], recv_sem=recv_sem.at[pair],
+            send_sem=part_send.at[pair], recv_sem=part_recv.at[pair],
             device_id=other, device_id_type=MESH,
         )
 
@@ -69,7 +97,6 @@
     col = iota((2 * tokens, tokens), 1)
     row = lax.rem(iota((2 * tokens, tokens), 0), tokens)
     allowed = (col <= row) & (lax.div(col, fresh_half) == core)
-    pl.semaphore_wait(barrier, 1)
 
     def sides(values):
         return jnp.where(low, values[:tokens], values[tokens:])
@@ -89,11 +116,10 @@
         parts[pair, 0] = sides(weighted)
         parts[pair, 1] = sides(jnp.broadcast_to(peak, spread))
         parts[pair, 2] = sides(jnp.broadcast_to(denom, spread))
-        to_other(pair).start()
         return carry
 
     def merge(pair, carry):
-        to_other(pair).wait()
+        to_other(pair).wait_recv()
         peak = jnp.maximum(parts[pair, 1], parts_in[pair, 1])
         left, right = jnp.exp(parts[pair, 1] - peak), jnp.exp(parts_in[pair, 1] - peak)
         denom = parts[pair, 2] * left + parts_in[pair, 2] * right
@@ -103,46 +129,13 @@
 
     each = pairs // pieces
     for piece in range(pieces):
-        for load in loads[piece]:
+        for load in early[piece]:
             load.wait()
         lax.fori_loop(piece * each, (piece + 1) * each, one_pair, 0)
-    lax.fori_loop(0, pairs, merge, 0)
-
-
-def expert_kernel(
-    peers, cap,
-    attn, resid, route_row, prob_row, gain, w_out, w_gate, w_up, w_down,
-    out,
-    wg, wu, wd, outgoing, arrived, results, returned, total, part, part_in, shuffle, shuffle_t,
-    copy_sem, wsend_sem, wrecv_sem, send_sem, recv_sem, back_send, back_recv, last_sem,
-):
-    me = lax.axis_index("expert")
-    core = lax.axis_index("seq")
-    other = {"seq": 1 - core}
-    tokens, width = attn.shape
-    blocks = width // LANES
-    slots = cap // 2
-    rows = slots * blocks
-    group_tokens = GROUP * slots
-    group_rows = GROUP * rows
-    groups = peers // GROUP
-    half = peers // 2
-
-    def ahead(rel):
-        return {"expert": lax.rem(me + rel, peers)}
-
-    barrier = pltpu.get_barrier_semaphore()
-    pl.semaphore_signal(barrier, inc=1, device_id=other, device_id_type=MESH)
-    for rel in range(1, peers):
-        pl.semaphore_signal(barrier, inc=1, device_id=ahead(rel), device_id_type=MESH)
-    loads = [
-        pltpu.make_async_copy(src, dst, copy_sem.at[i])
-        for i, (src, dst) in enumerate([
-            (w_gate, wg.at[0]), (w_up, wu.at[0]), (w_down, wd.at[0]),
-        ])
-    ]
     for load in loads:
         load.start()
+    for load in small:
+        load.wait()
 
     def place_of(rel):
         if isinstance(rel, int):
@@ -183,6 +176,10 @@
             [plain[j * group_tokens : (j + 1) * group_tokens] for j in range(blocks)], axis=1
         )
 
+    pl.semaphore_wait(barrier, peers)
+    for pair in range(pairs):
+        to_other(pair).start()
+    lax.fori_loop(0, pairs, merge, 0)
     hidden = (resid[...].astype(jnp.float32) + dot(attn[...], w_out[...])).astype(jnp.bfloat16)
     hidden_f = hidden.astype(jnp.float32)
     meansq = jnp.mean(hidden_f * hidden_f, axis=1, keepdims=True)
@@ -214,7 +211,6 @@
             device_id=ahead(peers - rel), device_id_type=MESH,
         )
 
-    pl.semaphore_wait(barrier, peers)
     by_place = sorted(range(1, peers), key=place_of)
     for rel in by_place:
         sent(rel).start()
@@ -279,7 +275,7 @@
     for rel in range(1, peers):
         sent(rel).wait_send()
         answered(rel).wait_send()
-    for copy in halves + [last]:
+    for copy in halves + [last] + [to_other(pair) for pair in range(pairs)]:
         copy.wait_send()
 
 
@@ -295,26 +291,6 @@
     cached = key_cache.shape[1]
     pairs = width // LANES
     bf16, f32 = jnp.bfloat16, jnp.float32
-    attn = pl.pallas_call(
-        attention_kernel,
-        name="attention",
-        out_shape=jax.ShapeDtypeStruct((tokens, width), bf16),
-        in_specs=[ANY] * 5,
-        out_specs=VMEM,
-        scratch_shapes=[
-            pltpu.VMEM((tokens, width), bf16),
-            pltpu.VMEM((cached, width), bf16),
-            pltpu.VMEM((cached, width), bf16),
-            pltpu.VMEM((tokens, width), bf16),
-            pltpu.VMEM((tokens, width), bf16),
-            pltpu.VMEM((pairs, 3, tokens, LANES), f32),
-            pltpu.VMEM((pairs, 3, tokens, LANES), f32),
-            pltpu.SemaphoreType.DMA((2, 5)),
-            pltpu.SemaphoreType.DMA((pairs,)),
-            pltpu.SemaphoreType.DMA((pairs,)),
-        ],
-        compiler_params=pltpu.CompilerParams(collective_id=1, has_side_effects=True),
-    )(query[0], key_cache[0], value_cache[0], key_new[0], value_new[0])
     cap = max(2, 3 * tokens // peers)
     slots = cap // 2
     total_rows = peers * slots * width // LANES
@@ -325,9 +301,26 @@
         functools.partial(expert_kernel, peers, cap),
         name="experts",
         out_shape=jax.ShapeDtypeStruct((tokens, width), bf16),
-        in_specs=[VMEM] * 6 + [ANY] * 3,
+        in_specs=[ANY] * 13,
         out_specs=VMEM,
         scratch_shapes=[
+            pltpu.VMEM((tokens, width), bf16),
+            pltpu.VMEM((1, tokens), jnp.int32),
+            pltpu.VMEM((1, tokens), f32),
+            pltpu.VMEM((1, width), f32),
+            pltpu.VMEM(out_weight.shape, bf16),
+            pltpu.SemaphoreType.DMA((5,)),
+            pltpu.VMEM((tokens, width), bf16),
+            pltpu.VMEM((cached, width), bf16),
+            pltpu.VMEM((cached, width), bf16),
+            pltpu.VMEM((tokens, width), bf16),
+            pltpu.VMEM((tokens, width), bf16),
+            pltpu.VMEM((pairs, 3, tokens, LANES), f32),
+            pltpu.VMEM((pairs, 3, tokens, LANES), f32),
+            pltpu.VMEM((tokens, width), bf16),
+            pltpu.SemaphoreType.DMA((2, 5)),
+            pltpu.SemaphoreType.DMA((pairs,)),
+            pltpu.SemaphoreType.DMA((pairs,)),
             pltpu.VMEM((2, width, hidden_units), bf16),
             pltpu.VMEM((2, width, hidden_units), bf16),
             pltpu.VMEM((2, hidden_units, width), bf16),
@@ -353,7 +346,8 @@
             collective_id=2, has_side_effects=True, vmem_limit_bytes=VMEM_GRANT
         ),
     )(
-        attn, resid[0], routing.reshape(1, tokens), router_prob, ffn_gain[None, :],
+        query[0], key_cache[0], value_cache[0], key_new[0], value_new[0],
+        resid[0], routing.reshape(1, tokens), router_prob, ffn_gain[None, :],
         out_weight, w_gate[0], w_up[0], w_down[0],
     )
     return result[None]

time: 115 us -> 112 us (0.974)
  Pallas kernels: 113 us -> 111 us
    pallas_call x1 -> x0, Pallas kernels: 28.1 us -> none  [on_device(): pl.pallas_call(attention_kernel, name='attention', out_shape=jax.ShapeDty...]
    pallas_call x1, Pallas kernels: 85.3 us -> 111 us  [on_device(): pl.pallas_call(functools.partial(expert_kernel, peers, cap), name='expert...]
where the time goes in v4:
time: 112 us
  Pallas kernels  111 us (99%)
  local copies, waits for them, and re-layouts  1.67 us (1%)
    pallas_call x1, Pallas kernels, on_device(): pl.pallas_call(functools.partial(expert_kernel, peers, cap), name='expert...  111 us

profile of v4, /device:TPU:37, one launch (start us, length us, event | category | flops | bytes accessed | tf_op | source)
XLA Modules:
  0.0 112.3 jit_solution(10281319905744826581)
XLA Ops:
  0.0 110.7 %experts.1 = bf16[128,1024]{1,0:T(8,128)(2,1)} custom-call(bf16[128,1024]{1,0:T(8,128)(2,1)} %bitcast.18, bf16[384,1024]{1,0:T(8,128)(2,1)} %bitcast.16, bf16[384,1024]{1,0:T(8,128)(2,1)} %bitcast.17, bf16[128,1024]{1,0:T(8,128)(2,1)} %bitcast.19, bf16[128,1024]{1,0:T(8,128)(2,1)} %bitcast.20, bf16[128,1024]{1,0:T(8,128)(2,1)} %bitcast.21, ...), custom_call_target="tpu_custom_call" | custom-call | tf_op jit(solution)/shard_map/experts/pallas_call | solution.py:300
  110.7 1.7 %copy.15 = bf16[1,128,1024]{2,1,0:T(8,128)(2,1)} copy(bf16[1,128,1024]{2,1,0:T(8,128)(2,1)} %bitcast.15) | data formatting | bytes 524288

commit v5 on v4

--- a/solution.py
+++ b/solution.py
@@ -185,35 +185,37 @@
     meansq = jnp.mean(hidden_f * hidden_f, axis=1, keepdims=True)
     normed = (hidden_f * lax.rsqrt(meansq + 1e-06) * gain[...]).astype(jnp.bfloat16)
 
+    def sent(rel):
+        n = place_of(rel)
+        spot = pl.ds(n * rows, rows)
+        return pltpu.make_async_remote_copy(
+            src_ref=outgoing.at[spot], dst_ref=arrived.at[spot], send_sem=send_sem.at[n], recv_sem=recv_sem.at[n],
+            device_id=ahead(rel), device_id_type=MESH,
+        )
+
+    def answered(rel):
+        n = place_of(rel)
+        spot = pl.ds(n * rows, rows)
+        return pltpu.make_async_remote_copy(
+            src_ref=results.at[spot], dst_ref=returned.at[spot], send_sem=back_send.at[n], recv_sem=back_recv.at[n],
+            device_id=ahead(peers - rel), device_id_type=MESH,
+        )
+
+    by_place = sorted(range(1, peers), key=place_of)
+    members = [[] for _ in range(groups)]
+    for rel in by_place:
+        members[place_of(rel) // GROUP].append(rel)
     for g in range(groups):
         picked = jnp.where(
             place_row == g * group_tokens + iota((group_tokens, tokens), 0), 1.0, 0.0
         ).astype(jnp.bfloat16)
         chosen = dot(picked, normed).astype(jnp.bfloat16)
         outgoing[pl.ds(g * group_rows, group_rows)] = pack(chosen)
+        for rel in members[g]:
+            sent(rel).start()
     own_place = place_of(0)
     own = pl.ds(own_place * rows, rows)
     arrived[own] = outgoing[own]
-
-    def sent(rel):
-        n = place_of(rel)
-        spot = pl.ds(n * rows, rows)
-        return pltpu.make_async_remote_copy(
-            src_ref=outgoing.at[spot], dst_ref=arrived.at[spot], send_sem=send_sem.at[n], recv_sem=recv_sem.at[n],
-            device_id=ahead(rel), device_id_type=MESH,
-        )
-
-    def answered(rel):
-        n = place_of(rel)
-        spot = pl.ds(n * rows, rows)
-        return pltpu.make_async_remote_copy(
-            src_ref=results.at[spot], dst_ref=returned.at[spot], send_sem=back_send.at[n], recv_sem=back_recv.at[n],
-            device_id=ahead(peers - rel), device_id_type=MESH,
-        )
-
-    by_place = sorted(range(1, peers), key=place_of)
-    for rel in by_place:
-        sent(rel).start()
     halves = [
         pltpu.make_async_remote_copy(
             src_ref=src, dst_ref=dst.at[1], send_sem=wsend_sem.at[i], recv_sem=wrecv_sem.at[i],
@@ -227,10 +229,6 @@
         load.wait()
     for copy in halves:
         copy.wait_recv()
-
-    members = [[] for _ in range(groups)]
-    for rel in by_place:
-        members[place_of(rel) // GROUP].append(rel)
 
     chunk = 2 * LANES
     chunks = wg.shape[2] // chunk

time: 112 us -> 112 us (level)
  no operation moved by 1% of the time
where the time goes in v5:
time: 112 us
  Pallas kernels  110 us (98%)
  local copies, waits for them, and re-layouts  1.67 us (1%)
    pallas_call x1, Pallas kernels, on_device(): pl.pallas_call(functools.partial(expert_kernel, peers, cap), name='expert...  110 us

profile of v5, /device:TPU:37, one launch (start us, length us, event | category | flops | bytes accessed | tf_op | source)
XLA Modules:
  0.0 111.8 jit_solution(10477449990178867409)
XLA Ops:
  0.0 110.1 %experts.1 = bf16[128,1024]{1,0:T(8,128)(2,1)} custom-call(bf16[128,1024]{1,0:T(8,128)(2,1)} %bitcast.18, bf16[384,1024]{1,0:T(8,128)(2,1)} %bitcast.16, bf16[384,1024]{1,0:T(8,128)(2,1)} %bitcast.17, bf16[128,1024]{1,0:T(8,128)(2,1)} %bitcast.19, bf16[128,1024]{1,0:T(8,128)(2,1)} %bitcast.20, bf16[128,1024]{1,0:T(8,128)(2,1)} %bitcast.21, ...), custom_call_target="tpu_custom_call" | custom-call | tf_op jit(solution)/shard_map/experts/pallas_call | solution.py:298
  110.1 1.7 %copy.15 = bf16[1,128,1024]{2,1,0:T(8,128)(2,1)} copy(bf16[1,128,1024]{2,1,0:T(8,128)(2,1)} %bitcast.15) | data formatting | bytes 524288
